TPU v7x, 32 devices: a whole 2x2x4 slice. The times are simulated.
32 devices in a mesh: section: 2 (over x), tensor: 8 (over z, core), dp: 2 (over y).
Axes of the slice: x: 2, y: 2, z: 4, core: 2. Of those that a mesh axis runs over, the one named last changes fastest.
Arguments:
- dec_queries: bfloat16 [2, 4, 512, 8192], P('section', 'dp', None, 'tensor'), may hold values from -8 to 8
- enc_keys: bfloat16 [2, 4, 512, 8192], P('section', 'dp', None, 'tensor'), may hold values from -4 to 4
- enc_values: bfloat16 [2, 4, 512, 8192], P('section', 'dp', None, 'tensor'), may hold values from -4 to 4
- out_grad: bfloat16 [2, 4, 512, 8192], P('section', 'dp', None, 'tensor'), may hold values from -15 to 15
- key_weight: bfloat16 [2, 1024, 8192], P('section', None, 'tensor'), may hold values from -0.1875 to 0.1875
- value_weight: bfloat16 [2, 1024, 8192], P('section', None, 'tensor'), may hold values from -0.1875 to 0.1875
- enc_hidden: float32 [4, 512, 1024], P('dp', 'section', 'tensor'), may hold values from -2 to 2, as said below
- enc_gain: float32 [1024], P('tensor'), may hold values from 0.1 to 1.9
Outputs:
- enc_input_grad: float32 [4, 512, 1024], P('dp', 'section', 'tensor')
Inputs may be any that keep to these rules, and one draw needn't show every extreme that they name: `enc_hidden`: every entry's magnitude is at least 0.25.
All inputs are finite; a program needn't handle non-finite values.
Results may differ from a plain program's by a relative error of at most 0.0041.
Values sent between devices are 32-bit elements; how exact they have to be, the bound alone decides.
A program may use at most 128 MiB of HBM per device.

v0:
```python
import functools

import jax
import jax.numpy as jnp
from jax import lax
from jax.experimental import pallas as pl
from jax.experimental.pallas import tpu as pltpu
from jax.sharding import PartitionSpec as P

DK = 128
CORES = 2
EPSILON = 1e-06
MESH = pl.DeviceIdType.MESH
F32 = jnp.float32
BF16 = jnp.bfloat16
QUERY_BLOCK = 256


def dot_nt(a, b, precision=None):
    return lax.dot_general(
        a, b, (((1,), (1,)), ((), ())), precision=precision, preferred_element_type=F32
    )


def dot_nn(a, b):
    return lax.dot_general(a, b, (((1,), (0,)), ((), ())), preferred_element_type=F32)


def dot_tn(a, b, precision=None):
    return lax.dot_general(
        a, b, (((0,), (0,)), ((), ())), precision=precision, preferred_element_type=F32
    )


def body(
    sections, tensors, query_block,
    q_hbm, k_hbm, v_hbm, g_hbm, wk_hbm, wv_hbm, hidden_hbm, gain_hbm,
    out_ref,
    q_buf, k_buf, v_buf, g_buf, w_buf, hidden, gain, grads,
    part, pair_in, section_in, line_out, line_in,
    square_out, square_in, cross_out, cross_in,
    load_sem, weight_sem, small_sem,
    pair_send, pair_recv, section_send, section_recv, line_send, line_recv,
    square_send, square_recv, cross_send, cross_recv,
):
    seqs, heads, dec_len, _ = q_buf.shape
    enc_len = k_buf.shape[2]
    inner = heads * DK
    model_width = w_buf.shape[0]
    feats = out_ref.shape[2]
    rows = out_ref.shape[1]
    chips = tensors // CORES
    s_me = lax.axis_index("section")
    t_me = lax.axis_index("tensor")
    z_me = lax.div(t_me, CORES)
    c_me = lax.rem(t_me, CORES)
    partner = z_me * CORES + (CORES - 1 - c_me)

    def loads(b, h):
        cols = pl.ds(pl.multiple_of(h * DK, DK), DK)
        return [
            pltpu.make_async_copy(src.at[0, b, :, cols], dst.at[b, h], load_sem.at[i, b, h])
            for i, (src, dst) in enumerate(
                ((q_hbm, q_buf), (k_hbm, k_buf), (v_hbm, v_buf), (g_hbm, g_buf))
            )
        ]

    def start_loads(b):
        def step(h, carry):
            for copy in loads(b, h):
                copy.start()
            return carry

        lax.fori_loop(0, heads, step, 0)

    weight_copies = [
        pltpu.make_async_copy(src.at[0], w_buf.at[:, pl.ds(i * inner, inner)], weight_sem.at[i])
        for i, src in enumerate((wk_hbm, wv_hbm))
    ]
    small_copies = [
        pltpu.make_async_copy(hidden_hbm, hidden, small_sem.at[0]),
        pltpu.make_async_copy(gain_hbm, gain, small_sem.at[1]),
    ]

    start_loads(0)
    for copy in small_copies + weight_copies:
        copy.start()
    for b in range(1, seqs):
        start_loads(b)

    barrier = pltpu.get_barrier_semaphore()
    for i in range(1, tensors):
        pl.semaphore_signal(
            barrier, inc=1, device_id={"tensor": lax.rem(t_me + i, tensors)}, device_id_type=MESH
        )
    for i in range(1, sections):
        pl.semaphore_signal(
            barrier, inc=1, device_id={"section": lax.rem(s_me + i, sections)}, device_id_type=MESH
        )

    def head(b, h):
        for copy in loads(b, h):
            copy.wait()
        keys = k_buf[b, h]
        values = v_buf[b, h]
        key_grad = None
        for start in range(0, dec_len, query_block):
            queries = q_buf[b, h, pl.ds(start, query_block), :]
            out_grads = g_buf[b, h, pl.ds(start, query_block), :]
            scores = dot_nt(keys, queries)
            shifted = jnp.exp(scores - jnp.max(scores, axis=0, keepdims=True))
            probs = shifted * (1.0 / jnp.sum(shifted, axis=0, keepdims=True))
            probs_low = probs.astype(BF16)
            prob_grad = dot_nt(values, out_grads)
            row_dot = jnp.sum(probs_low.astype(F32) * prob_grad, axis=0, keepdims=True)
            score_low = (probs * (prob_grad - row_dot)).astype(BF16)
            value_term = dot_nn(probs_low, out_grads)
            key_term = dot_nn(score_low, queries)
            if key_grad is None:
                key_grad, value_grad = key_term, value_term
            else:
                key_grad, value_grad = key_grad + key_term, value_grad + value_term
        grads[:, pl.ds(pl.multiple_of(h * DK, DK), DK)] = key_grad.astype(BF16)
        grads[:, pl.ds(pl.multiple_of(inner + h * DK, DK), DK)] = value_grad.astype(BF16)

    def pair_copy(b, k):
        return pltpu.make_async_remote_copy(
            src_ref=part.at[b, k, CORES - 1 - c_me], dst_ref=pair_in.at[b, k],
            send_sem=pair_send.at[b, k], recv_sem=pair_recv.at[b, k],
            device_id={"tensor": partner}, device_id_type=MESH,
        )

    def section_copies(b, k):
        copies = []
        for i in range(1, sections):
            target = lax.rem(s_me + i, sections)
            copies.append(pltpu.make_async_remote_copy(
                src_ref=part.at[b, k, c_me, target], dst_ref=section_in.at[b, k, i - 1],
                send_sem=section_send.at[b, k, i - 1], recv_sem=section_recv.at[b, k, i - 1],
                device_id={"section": target}, device_id_type=MESH,
            ))
        return copies

    def line_copy(b, k):
        target = lax.rem(z_me + 1 + k, chips) * CORES + c_me
        return pltpu.make_async_remote_copy(
            src_ref=line_out.at[b, k], dst_ref=line_in.at[b, k],
            send_sem=line_send.at[b, k], recv_sem=line_recv.at[b, k],
            device_id={"tensor": target}, device_id_type=MESH,
        )

    def stat_copies(src, dst, send, recv):
        return [
            pltpu.make_async_remote_copy(
                src_ref=src, dst_ref=dst.at[i - 1],
                send_sem=send.at[i - 1], recv_sem=recv.at[i - 1],
                device_id={"tensor": lax.rem(t_me + i, tensors)}, device_id_type=MESH,
            )
            for i in range(1, tensors)
        ]

    def square_copies():
        return stat_copies(square_out, square_in, square_send, square_recv)

    def cross_copies(b):
        return stat_copies(
            cross_out.at[b], cross_in.at[b], cross_send.at[b], cross_recv.at[b]
        )

    def lane_sums(x):
        total = dot_nt(jnp.ones((8, feats), F32), x, lax.Precision.HIGHEST)
        return total[0:1, :]

    def spread(row):
        return dot_tn(
            jnp.broadcast_to(row, (8, rows)), jnp.full((8, feats), 0.125, F32),
            lax.Precision.HIGHEST,
        )

    def project(b, k):
        chip = lax.rem(z_me + 1 + k, chips)
        width = CORES * feats
        block = dot_nt(
            grads[...], w_buf[pl.ds(pl.multiple_of(chip * width, width), width), :]
        )
        for half in range(CORES):
            part[b, k, half] = block[:, half * feats : (half + 1) * feats].reshape(
                sections, rows, feats
            )
        pair_copy(b, k).start()

    def pair_step(b, k):
        pair_copy(b, k).wait_recv()
        part[b, k, c_me] = part[b, k, c_me] + pair_in[b, k]
        for copy in section_copies(b, k):
            copy.start()

    def section_step(b, k):
        total = part[b, k, c_me, s_me]
        for i, copy in enumerate(section_copies(b, k)):
            copy.wait_recv()
            total = total + section_in[b, k, i]
        line_out[b, k] = total

    def loop(low, high, step):
        def run(i, carry):
            step(i)
            return carry

        lax.fori_loop(low, high, run, 0)

    def forward(b, k):
        section_step(b, k)
        line_copy(b, k).start()

    def finish_sum(b):
        section_step(b, chips - 1)
        total = line_out[b, chips - 1]
        for k in range(chips - 1):
            line_copy(b, k).wait_recv()
            total = total + line_in[b, k]
        scaled = gain[...] * total
        out_ref[b] = scaled
        cross_out[b] = lane_sums(scaled * hidden[b])
        for copy in cross_copies(b):
            copy.start()

    def finish_norm(b):
        for copy in cross_copies(b):
            copy.wait_recv()
        cross = cross_out[b]
        square = square_out[b]
        for i in range(tensors - 1):
            cross = cross + cross_in[b, i]
            square = square + square_in[i, b]
        inverse = lax.rsqrt(square / model_width + EPSILON)
        factor = cross * inverse * inverse * inverse / model_width
        out_ref[b] = out_ref[b] * spread(inverse) - hidden[b] * spread(factor)

    heads_per_step = heads // chips
    for b in range(seqs):
        def heads_step(k):
            loop(0, heads_per_step, lambda i: head(b, k * heads_per_step + i))
            if b > 0:
                @pl.when(k < chips - 1)
                def _():
                    forward(b - 1, k)

        if b == 0:
            loop(0, heads, lambda h: head(b, h))
            for copy in small_copies:
                copy.wait()
            for i in range(seqs):
                square_out[i] = lane_sums(hidden[i] * hidden[i])
            for copy in weight_copies:
                copy.wait()
            pl.semaphore_wait(barrier, tensors - 1 + sections - 1)
            for copy in square_copies():
                copy.start()
        else:
            loop(0, chips, heads_step)

        project(b, 0)

        def project_step(k):
            project(b, k)
            pair_step(b, k - 1)

        loop(1, chips, project_step)
        pair_step(b, chips - 1)

    for copy in square_copies():
        copy.wait_recv()
    for b in range(seqs - 1):
        finish_sum(b)
    loop(0, chips - 1, lambda k: forward(seqs - 1, k))
    finish_sum(seqs - 1)
    for b in range(seqs):
        finish_norm(b)

    for copy in square_copies():
        copy.wait_send()
    for b in range(seqs):
        for copy in cross_copies(b):
            copy.wait_send()

        def drain(k):
            pair_copy(b, k).wait_send()
            for copy in section_copies(b, k):
                copy.wait_send()

        loop(0, chips, drain)
        loop(0, chips - 1, lambda k: line_copy(b, k).wait_send())


def per_device(
    sections, tensors,
    dec_queries, enc_keys, enc_values, out_grad, key_weight, value_weight, enc_hidden, enc_gain,
):
    _, seqs, dec_len, inner = dec_queries.shape
    enc_len = enc_keys.shape[2]
    heads = inner // DK
    model_width = key_weight.shape[1]
    chips = tensors // CORES
    feats = model_width // tensors
    rows = enc_len // sections
    dma = pltpu.SemaphoreType.DMA
    call = pl.pallas_call(
        functools.partial(body, sections, tensors, min(QUERY_BLOCK, dec_len)),
        out_shape=jax.ShapeDtypeStruct((seqs, rows, feats), F32),
        in_specs=[pl.BlockSpec(memory_space=pl.ANY)] * 8,
        out_specs=pl.BlockSpec(memory_space=pltpu.VMEM),
        scratch_shapes=[
            pltpu.VMEM((seqs, heads, dec_len, DK), BF16),
            pltpu.VMEM((seqs, heads, enc_len, DK), BF16),
            pltpu.VMEM((seqs, heads, enc_len, DK), BF16),
            pltpu.VMEM((seqs, heads, dec_len, DK), BF16),
            pltpu.VMEM((model_width, 2 * inner), BF16),
            pltpu.VMEM((seqs, rows, feats), F32),
            pltpu.VMEM((1, feats), F32),
            pltpu.VMEM((enc_len, 2 * inner), BF16),
            pltpu.VMEM((seqs, chips, CORES, sections, rows, feats), F32),
            pltpu.VMEM((seqs, chips, sections, rows, feats), F32),
            pltpu.VMEM((seqs, chips, sections - 1, rows, feats), F32),
            pltpu.VMEM((seqs, chips, rows, feats), F32),
            pltpu.VMEM((seqs, chips - 1, rows, feats), F32),
            pltpu.VMEM((seqs, 1, rows), F32),
            pltpu.VMEM((tensors - 1, seqs, 1, rows), F32),
            pltpu.VMEM((seqs, 1, rows), F32),
            pltpu.VMEM((seqs, tensors - 1, 1, rows), F32),
            dma((4, seqs, heads)),
            dma((2,)),
            dma((2,)),
            dma((seqs, chips)),
            dma((seqs, chips)),
            dma((seqs, chips, sections - 1)),
            dma((seqs, chips, sections - 1)),
            dma((seqs, chips - 1)),
            dma((seqs, chips - 1)),
            dma((tensors - 1,)),
            dma((tensors - 1,)),
            dma((seqs, tensors - 1)),
            dma((seqs, tensors - 1)),
        ],
        compiler_params=pltpu.CompilerParams(
            collective_id=0, has_side_effects=True, vmem_limit_bytes=60 * 1024 * 1024
        ),
    )
    return call(
        dec_queries, enc_keys, enc_values, out_grad, key_weight, value_weight,
        enc_hidden, enc_gain.reshape(1, feats),
    )


def solution(mesh):
    wide = P("section", "dp", None, "tensor")
    return jax.shard_map(
        functools.partial(per_device, mesh.shape["section"], mesh.shape["tensor"]),
        mesh=mesh,
        in_specs=(
            wide, wide, wide, wide,
            P("section", None, "tensor"),
            P("section", None, "tensor"),
            P("dp", "section", "tensor"),
            P("tensor"),
        ),
        out_specs=P("dp", "section", "tensor"),
        check_vma=False,
    )
```

profile of v0, /device:TPU:0, one launch (start us, length us, event | category | flops | bytes accessed | tf_op | source)
XLA Modules:
  0.0 57.8 jit_solution(17586706662473367624)
XLA Ops:
  0.0 56.1 %shard_map.82 = f32[2,256,128]{2,1,0:T(8,128)} custom-call(bf16[1,2,512,1024]{3,2,1,0:T(8,128)(2,1)} %q_hbm.1, bf16[1,2,512,1024]{3,2,1,0:T(8,128)(2,1)} %k_hbm.1, bf16[1,2,512,1024]{3,2,1,0:T(8,128)(2,1)} %v_hbm.1, bf16[1,2,512,1024]{3,2,1,0:T(8,128)(2,1)} %g_hbm.1, bf16[1,1024,1024]{2,1,0:T(8,128)(2,1)} %wk_hbm.1, bf16[1,1024,1024]{2,1,0:T(8,128)(2,1)} %wv_hbm.1, ...), custom_call_target="tpu_custom_call" | custom-call | tf_op jit(solution)/shard_map/pallas_call | solution.py:349
  56.1 1.7 %copy.10 = f32[2,256,128]{2,1,0:T(8,128)} copy(f32[2,256,128]{2,1,0:T(8,128)} %shard_map.82) | data formatting | bytes 524288
where the time goes:
time: 57.9 us; the launch traced here: 57.8 us
  Pallas kernels  56.1 us (97%)
  local copies, waits for them, and re-layouts  1.67 us (3%)
    pallas_call x1, Pallas kernels, per_device(): call(dec_queries, enc_keys, enc_values, out_grad, key_weight, value_weigh...  56.1 us
    unnamed x1, local copies, waits for them, and re-layouts  1.67 us

commit v1 on v0

v1 whole, which is shorter than its diff:
```python
import functools

import jax
import jax.numpy as jnp
from jax import lax
from jax.experimental import pallas as pl
from jax.experimental.pallas import tpu as pltpu
from jax.sharding import PartitionSpec as P

DK = 128
CORES = 2
EPSILON = 1e-06
MESH = pl.DeviceIdType.MESH
F32 = jnp.float32
BF16 = jnp.bfloat16
QUERY_BLOCK = 256
PIECES = 2


def dot_nt(a, b, precision=None):
    return lax.dot_general(
        a, b, (((1,), (1,)), ((), ())), precision=precision, preferred_element_type=F32
    )


def dot_nn(a, b):
    return lax.dot_general(a, b, (((1,), (0,)), ((), ())), preferred_element_type=F32)


def dot_tn(a, b, precision=None):
    return lax.dot_general(
        a, b, (((0,), (0,)), ((), ())), precision=precision, preferred_element_type=F32
    )


def body(
    sections, tensors, query_block,
    q_hbm, k_hbm, v_hbm, g_hbm, wk_hbm, wv_hbm, hidden_hbm, gain_hbm,
    out_ref,
    q_buf, k_buf, v_buf, g_buf, w_buf, hidden, gain, grads,
    scores_even, prob_grad_even, peak_even, scores_odd, prob_grad_odd, peak_odd,
    part, pair_in, section_in, line_out, line_in,
    square_out, square_in, cross_out, cross_in, inverse_wide, hidden_scaled,
    load_sem, weight_sem, small_sem,
    pair_send, pair_recv, section_send, section_recv, line_send, line_recv,
    square_send, square_recv, cross_send, cross_recv,
):
    seqs, heads, dec_len, _ = q_buf.shape
    enc_len = k_buf.shape[2]
    inner = heads * DK
    model_width = w_buf.shape[0]
    feats = out_ref.shape[2]
    rows = out_ref.shape[1]
    chips = tensors // CORES
    s_me = lax.axis_index("section")
    t_me = lax.axis_index("tensor")
    z_me = lax.div(t_me, CORES)
    c_me = lax.rem(t_me, CORES)
    partner = z_me * CORES + (CORES - 1 - c_me)
    pieces = PIECES
    piece_rows = rows // pieces

    def loads(b, h):
        cols = pl.ds(pl.multiple_of(h * DK, DK), DK)
        return [
            pltpu.make_async_copy(src.at[0, b, :, cols], dst.at[b, h], load_sem.at[i, b, h])
            for i, (src, dst) in enumerate(
                ((q_hbm, q_buf), (k_hbm, k_buf), (v_hbm, v_buf), (g_hbm, g_buf))
            )
        ]

    def start_loads(b):
        def step(h, carry):
            for copy in loads(b, h):
                copy.start()
            return carry

        lax.fori_loop(0, heads, step, 0)

    weight_copies = [
        pltpu.make_async_copy(src.at[0], w_buf.at[:, pl.ds(i * inner, inner)], weight_sem.at[i])
        for i, src in enumerate((wk_hbm, wv_hbm))
    ]
    small_copies = [
        pltpu.make_async_copy(hidden_hbm, hidden, small_sem.at[0]),
        pltpu.make_async_copy(gain_hbm, gain, small_sem.at[1]),
    ]

    start_loads(0)
    for copy in small_copies + weight_copies:
        copy.start()
    for b in range(1, seqs):
        start_loads(b)

    barrier = pltpu.get_barrier_semaphore()
    for i in range(1, tensors):
        pl.semaphore_signal(
            barrier, inc=1, device_id={"tensor": lax.rem(t_me + i, tensors)}, device_id_type=MESH
        )
    for i in range(1, sections):
        pl.semaphore_signal(
            barrier, inc=1, device_id={"section": lax.rem(s_me + i, sections)}, device_id_type=MESH
        )

    blocks = dec_len // query_block

    def wait_loads(i):
        for copy in loads(lax.div(i, heads), lax.rem(i, heads)):
            copy.wait()

    def score_step(i, bufs):
        scores_buf, prob_grad_buf, peak_buf = bufs
        b, h = lax.div(i, heads), lax.rem(i, heads)
        keys = k_buf[b, h]
        values = v_buf[b, h]
        for n in range(blocks):
            span = pl.ds(n * query_block, query_block)
            scores = dot_nt(keys, q_buf[b, h, span, :])
            scores_buf[n] = scores
            peak_buf[n] = jnp.max(scores, axis=0, keepdims=True)
            prob_grad_buf[n] = dot_nt(values, g_buf[b, h, span, :])

    def grad_step(i, bufs):
        scores_buf, prob_grad_buf, peak_buf = bufs
        b, h = lax.div(i, heads), lax.rem(i, heads)
        key_grad = None
        for n in range(blocks):
            span = pl.ds(n * query_block, query_block)
            shifted = jnp.exp(scores_buf[n] - peak_buf[n])
            scale = 1.0 / jnp.sum(shifted, axis=0, keepdims=True)
            probs_low = (shifted * scale).astype(BF16)
            row_dot = jnp.sum(probs_low.astype(F32) * prob_grad_buf[n], axis=0, keepdims=True)
            score_low = probs_low * (prob_grad_buf[n] - row_dot).astype(BF16)
            value_term = dot_nn(probs_low, g_buf[b, h, span, :])
            key_term = dot_nn(score_low, q_buf[b, h, span, :])
            if key_grad is None:
                key_grad, value_grad = key_term, value_term
            else:
                key_grad, value_grad = key_grad + key_term, value_grad + value_term
        grads[:, pl.ds(pl.multiple_of(h * DK, DK), DK)] = key_grad.astype(BF16)
        grads[:, pl.ds(pl.multiple_of(inner + h * DK, DK), DK)] = value_grad.astype(BF16)

    even = (scores_even, prob_grad_even, peak_even)
    odd = (scores_odd, prob_grad_odd, peak_odd)

    def head_pair(i):
        wait_loads(i + 1)
        score_step(i + 1, odd)
        grad_step(i, even)
        following = jnp.minimum(i + 2, seqs * heads - 1)

        @pl.when(i + 2 < seqs * heads)
        def _():
            wait_loads(i + 2)

        score_step(following, even)
        grad_step(i + 1, odd)

    def order(j):
        if chips & (chips - 1):
            return lax.rem(z_me + 1 + j, chips)
        chip, unit = 0, 1
        while unit < chips:
            bits = lax.div(z_me, unit) + lax.div(chips - 1 - j, unit)
            chip = chip + unit * lax.rem(bits, 2)
            unit *= 2
        return chip

    def section_of(i):
        return lax.rem(s_me + i, sections)

    def piece(r):
        return pl.ds(r * piece_rows, piece_rows)

    def pair_copy(b, i, j):
        return pltpu.make_async_remote_copy(
            src_ref=part.at[b, i, j, CORES - 1 - c_me], dst_ref=pair_in.at[b, i, j],
            send_sem=pair_send.at[b, i, j], recv_sem=pair_recv.at[b, i, j],
            device_id={"tensor": partner}, device_id_type=MESH,
        )

    def section_copy(b, i, j, r):
        return pltpu.make_async_remote_copy(
            src_ref=part.at[b, i, j, c_me, piece(r)], dst_ref=section_in.at[b, i - 1, j, piece(r)],
            send_sem=section_send.at[b, i - 1, j, r], recv_sem=section_recv.at[b, i - 1, j, r],
            device_id={"section": section_of(i)}, device_id_type=MESH,
        )

    def line_copy(b, j, r):
        return pltpu.make_async_remote_copy(
            src_ref=line_out.at[b, j, piece(r)], dst_ref=line_in.at[b, j, piece(r)],
            send_sem=line_send.at[b, j, r], recv_sem=line_recv.at[b, j, r],
            device_id={"tensor": order(j) * CORES + c_me}, device_id_type=MESH,
        )

    def stat_copies(src, dst, send, recv):
        return [
            pltpu.make_async_remote_copy(
                src_ref=src, dst_ref=dst.at[i - 1],
                send_sem=send.at[i - 1], recv_sem=recv.at[i - 1],
                device_id={"tensor": lax.rem(t_me + i, tensors)}, device_id_type=MESH,
            )
            for i in range(1, tensors)
        ]

    def square_copies():
        return stat_copies(square_out, square_in, square_send, square_recv)

    def cross_copies(b):
        return stat_copies(
            cross_out.at[b], cross_in.at[b], cross_send.at[b], cross_recv.at[b]
        )

    def lane_sums(x):
        total = dot_nt(jnp.ones((8, feats), F32), x, lax.Precision.HIGHEST)
        return total[0:1, :]

    def spread(row):
        return dot_tn(
            jnp.broadcast_to(row, (8, rows)), jnp.full((8, feats), 0.125, F32),
            lax.Precision.HIGHEST,
        )

    def loop(low, high, step):
        def run(i, carry):
            step(i)
            return carry

        lax.fori_loop(low, high, run, 0)

    def project(b, i, j):
        width = CORES * feats
        block = dot_nt(
            grads[pl.ds(pl.multiple_of(section_of(i) * rows, rows), rows), :],
            w_buf[pl.ds(pl.multiple_of(order(j) * width, width), width), :],
        )
        for half in range(CORES):
            part[b, i, j, half] = block[:, half * feats : (half + 1) * feats]
        pair_copy(b, i, j).start()

    def send_section(b, i, j):
        pair_copy(b, i, j).wait_recv()
        for r in range(pieces):
            part[b, i, j, c_me, piece(r)] += pair_in[b, i, j, piece(r)]
            section_copy(b, i, j, r).start()

    def project_all(b):
        for i in range(1, sections):
            project(b, i, 0)

            def step(j):
                project(b, i, j)
                send_section(b, i, j - 1)

            loop(1, chips, step)
            if i + 1 < sections:
                send_section(b, i, chips - 1)
        project(b, 0, 0)
        send_section(b, sections - 1, chips - 1)
        loop(1, chips, lambda j: project(b, 0, j))

    def gather_section(b, j):
        pair_copy(b, 0, j).wait_recv()
        for r in range(pieces):
            total = part[b, 0, j, c_me, piece(r)] + pair_in[b, 0, j, piece(r)]
            for i in range(1, sections):
                section_copy(b, i, j, r).wait_recv()
                total = total + section_in[b, i - 1, j, piece(r)]
            line_out[b, j, piece(r)] = total

            @pl.when(j < chips - 1)
            def _():
                line_copy(b, j, r).start()

    def finish_sum(b):
        for r in range(pieces):
            total = line_out[b, chips - 1, piece(r)]
            for j in range(chips - 1):
                line_copy(b, j, r).wait_recv()
                total = total + line_in[b, j, piece(r)]
            out_ref[b, piece(r)] = gain[...] * total
        cross_out[b] = lane_sums(out_ref[b] * hidden[b])
        for copy in cross_copies(b):
            copy.start()
        out_ref[b] = out_ref[b] * inverse_wide[b]

    def prepare_norm():
        for copy in square_copies():
            copy.wait_recv()
        for b in range(seqs):
            square = square_out[b]
            for i in range(tensors - 1):
                square = square + square_in[i, b]
            inverse = lax.rsqrt(square / model_width + EPSILON)
            inverse_wide[b] = spread(inverse)
            hidden_scaled[b] = hidden[b] * spread(inverse * inverse * inverse / model_width)

    def finish_norm(b):
        cross = cross_out[b]
        for i, copy in enumerate(cross_copies(b)):
            copy.wait_recv()
            cross = cross + cross_in[b, i]
        out_ref[b] = out_ref[b] - hidden_scaled[b] * spread(cross)

    steps = heads // 2
    wait_loads(0)
    score_step(0, even)
    for b in range(seqs):
        def heads_step(j):
            head_pair(b * heads + 2 * j)
            if b > 0:
                @pl.when((j > 0) & (j <= chips))
                def _():
                    gather_section(b - 1, j - 1)

        loop(0, steps, heads_step)
        if b == 0:
            for copy in small_copies:
                copy.wait()
            for copy in weight_copies:
                copy.wait()
            pl.semaphore_wait(barrier, tensors - 1 + sections - 1)
        project_all(b)
        if b == 0:
            for i in range(seqs):
                square_out[i] = lane_sums(hidden[i] * hidden[i])
            for copy in square_copies():
                copy.start()
        else:
            for j in range(min(steps - 1, chips), chips):
                gather_section(b - 1, j)
    prepare_norm()
    last = seqs - 1
    loop(0, chips // 2, lambda j: gather_section(last, j))
    for b in range(seqs - 1):
        finish_sum(b)
    loop(chips // 2, chips, lambda j: gather_section(last, j))
    finish_sum(last)
    for b in range(seqs):
        finish_norm(b)

    for copy in square_copies():
        copy.wait_send()
    for b in range(seqs):
        for copy in cross_copies(b):
            copy.wait_send()

        def drain(j):
            for i in range(sections):
                pair_copy(b, i, j).wait_send()
                for r in range(pieces if i else 0):
                    section_copy(b, i, j, r).wait_send()

        def drain_line(j):
            for r in range(pieces):
                line_copy(b, j, r).wait_send()

        loop(0, chips, drain)
        loop(0, chips - 1, drain_line)


def per_device(
    sections, tensors,
    dec_queries, enc_keys, enc_values, out_grad, key_weight, value_weight, enc_hidden, enc_gain,
):
    _, seqs, dec_len, inner = dec_queries.shape
    enc_len = enc_keys.shape[2]
    heads = inner // DK
    model_width = key_weight.shape[1]
    chips = tensors // CORES
    feats = model_width // tensors
    rows = enc_len // sections
    dma = pltpu.SemaphoreType.DMA
    query_block = min(QUERY_BLOCK, dec_len)
    blocks = dec_len // query_block
    unit = [
        pltpu.VMEM((blocks, enc_len, query_block), F32),
        pltpu.VMEM((blocks, enc_len, query_block), F32),
        pltpu.VMEM((blocks, 1, query_block), F32),
    ]
    call = pl.pallas_call(
        functools.partial(body, sections, tensors, query_block),
        out_shape=jax.ShapeDtypeStruct((seqs, rows, feats), F32),
        in_specs=[pl.BlockSpec(memory_space=pl.ANY)] * 8,
        out_specs=pl.BlockSpec(memory_space=pltpu.VMEM),
        scratch_shapes=[
            pltpu.VMEM((seqs, heads, dec_len, DK), BF16),
            pltpu.VMEM((seqs, heads, enc_len, DK), BF16),
            pltpu.VMEM((seqs, heads, enc_len, DK), BF16),
            pltpu.VMEM((seqs, heads, dec_len, DK), BF16),
            pltpu.VMEM((model_width, 2 * inner), BF16),
            pltpu.VMEM((seqs, rows, feats), F32),
            pltpu.VMEM((1, feats), F32),
            pltpu.VMEM((enc_len, 2 * inner), BF16),
            *unit, *unit,
            pltpu.VMEM((seqs, sections, chips, CORES, rows, feats), F32),
            pltpu.VMEM((seqs, sections, chips, rows, feats), F32),
            pltpu.VMEM((seqs, sections - 1, chips, rows, feats), F32),
            pltpu.VMEM((seqs, chips, rows, feats), F32),
            pltpu.VMEM((seqs, chips - 1, rows, feats), F32),
            pltpu.VMEM((seqs, 1, rows), F32),
            pltpu.VMEM((tensors - 1, seqs, 1, rows), F32),
            pltpu.VMEM((seqs, 1, rows), F32),
            pltpu.VMEM((seqs, tensors - 1, 1, rows), F32),
            pltpu.VMEM((seqs, rows, feats), F32),
            pltpu.VMEM((seqs, rows, feats), F32),
            dma((4, seqs, heads)),
            dma((2,)),
            dma((2,)),
            dma((seqs, sections, chips)),
            dma((seqs, sections, chips)),
            dma((seqs, sections - 1, chips, PIECES)),
            dma((seqs, sections - 1, chips, PIECES)),
            dma((seqs, chips - 1, PIECES)),
            dma((seqs, chips - 1, PIECES)),
            dma((tensors - 1,)),
            dma((tensors - 1,)),
            dma((seqs, tensors - 1)),
            dma((seqs, tensors - 1)),
        ],
        compiler_params=pltpu.CompilerParams(
            collective_id=0, has_side_effects=True, vmem_limit_bytes=60 * 1024 * 1024
        ),
    )
    return call(
        dec_queries, enc_keys, enc_values, out_grad, key_weight, value_weight,
        enc_hidden, enc_gain.reshape(1, feats),
    )


def solution(mesh):
    wide = P("section", "dp", None, "tensor")
    return jax.shard_map(
        functools.partial(per_device, mesh.shape["section"], mesh.shape["tensor"]),
        mesh=mesh,
        in_specs=(
            wide, wide, wide, wide,
            P("section", None, "tensor"),
            P("section", None, "tensor"),
            P("dp", "section", "tensor"),
            P("tensor"),
        ),
        out_specs=P("dp", "section", "tensor"),
        check_vma=False,
    )
```

time: 57.9 us -> 52.5 us (0.907)
  Pallas kernels: 56.1 us -> 50.7 us
    pallas_call x1, Pallas kernels: 56.1 us -> 50.7 us  [per_device(): call(dec_queries, enc_keys, enc_values, out_grad, key_weight, value_weigh...]
where the time goes in v1:
time: 52.5 us; the launch traced here: 52.4 us
  Pallas kernels  50.7 us (97%)
  local copies, waits for them, and re-layouts  1.67 us (3%)
    pallas_call x1, Pallas kernels, per_device(): call(dec_queries, enc_keys, enc_values, out_grad, key_weight, value_weigh...  50.7 us
    unnamed x1, local copies, waits for them, and re-layouts  1.67 us

profile of v1, /device:TPU:0, one launch (start us, length us, event | category | flops | bytes accessed | tf_op | source)
XLA Modules:
  0.0 52.4 jit_solution(13216362949719604841)
XLA Ops:
  0.0 50.7 %shard_map.82 = f32[2,256,128]{2,1,0:T(8,128)} custom-call(bf16[1,2,512,1024]{3,2,1,0:T(8,128)(2,1)} %q_hbm.1, bf16[1,2,512,1024]{3,2,1,0:T(8,128)(2,1)} %k_hbm.1, bf16[1,2,512,1024]{3,2,1,0:T(8,128)(2,1)} %v_hbm.1, bf16[1,2,512,1024]{3,2,1,0:T(8,128)(2,1)} %g_hbm.1, bf16[1,1024,1024]{2,1,0:T(8,128)(2,1)} %wk_hbm.1, bf16[1,1024,1024]{2,1,0:T(8,128)(2,1)} %wv_hbm.1, ...), custom_call_target="tpu_custom_call" | custom-call | tf_op jit(solution)/shard_map/pallas_call | solution.py:425
  50.7 1.7 %copy.10 = f32[2,256,128]{2,1,0:T(8,128)} copy(f32[2,256,128]{2,1,0:T(8,128)} %shard_map.82) | data formatting | bytes 524288

commit v2 on v1

v2 whole, which is shorter than its diff:
```python
import functools

import jax
import jax.numpy as jnp
from jax import lax
from jax.experimental import pallas as pl
from jax.experimental.pallas import tpu as pltpu
from jax.sharding import PartitionSpec as P

DK = 128
CORES = 2
EPSILON = 1e-06
MESH = pl.DeviceIdType.MESH
F32 = jnp.float32
BF16 = jnp.bfloat16
QUERY_BLOCK = 256
PIECES = 4


def dot_nt(a, b, precision=None):
    return lax.dot_general(
        a, b, (((1,), (1,)), ((), ())), precision=precision, preferred_element_type=F32
    )


def dot_nn(a, b):
    return lax.dot_general(a, b, (((1,), (0,)), ((), ())), preferred_element_type=F32)


def dot_tn(a, b, precision=None):
    return lax.dot_general(
        a, b, (((0,), (0,)), ((), ())), precision=precision, preferred_element_type=F32
    )


def body(
    sections, tensors, query_block,
    q_hbm, k_hbm, v_hbm, g_hbm, wk_hbm, wv_hbm, hidden_hbm, gain_hbm,
    out_ref,
    qg_buf, kv_buf, w_buf, hidden, gain, grads,
    scores_even, prob_grad_even, peak_even, scores_odd, prob_grad_odd, peak_odd,
    part, pair_in, section_in, line_out, line_in,
    square_out, square_in, cross_out, cross_in, inverse_wide, hidden_scaled,
    load_sem, weight_sem, small_sem,
    pair_send, pair_recv, section_send, section_recv, line_send, line_recv,
    square_send, square_recv, cross_send, cross_recv,
):
    seqs, heads, _, dec_len, _ = qg_buf.shape
    enc_len = kv_buf.shape[3]
    inner = heads * DK
    model_width = w_buf.shape[0]
    feats = out_ref.shape[2]
    rows = out_ref.shape[1]
    chips = tensors // CORES
    s_me = lax.axis_index("section")
    t_me = lax.axis_index("tensor")
    z_me = lax.div(t_me, CORES)
    c_me = lax.rem(t_me, CORES)
    partner = z_me * CORES + (CORES - 1 - c_me)
    pieces = PIECES
    at_end = (z_me == 0) | (z_me == chips - 1)
    piece_rows = rows // pieces

    def loads(b, h):
        cols = pl.ds(pl.multiple_of(h * DK, DK), DK)
        return [
            pltpu.make_async_copy(src.at[0, b, :, cols], dst.at[b, h, n], load_sem.at[i, b, h])
            for i, (sources, dst) in enumerate((((q_hbm, g_hbm), qg_buf), ((k_hbm, v_hbm), kv_buf)))
            for n, src in enumerate(sources)
        ]

    def settle(ref, sem):
        pltpu.make_async_copy(ref, ref, sem).wait()

    def start_loads(b):
        def step(h, carry):
            for copy in loads(b, h):
                copy.start()
            return carry

        lax.fori_loop(0, heads, step, 0)

    weight_copies = [
        pltpu.make_async_copy(src.at[0], w_buf.at[:, pl.ds(i * inner, inner)], weight_sem)
        for i, src in enumerate((wk_hbm, wv_hbm))
    ]
    small_copies = [
        pltpu.make_async_copy(hidden_hbm, hidden, small_sem.at[0]),
        pltpu.make_async_copy(gain_hbm, gain, small_sem.at[1]),
    ]

    start_loads(0)
    for copy in small_copies + weight_copies:
        copy.start()
    for b in range(1, seqs):
        start_loads(b)

    barrier = pltpu.get_barrier_semaphore()
    for i in range(1, tensors):
        pl.semaphore_signal(
            barrier, inc=1, device_id={"tensor": lax.rem(t_me + i, tensors)}, device_id_type=MESH
        )
    for i in range(1, sections):
        pl.semaphore_signal(
            barrier, inc=1, device_id={"section": lax.rem(s_me + i, sections)}, device_id_type=MESH
        )

    blocks = dec_len // query_block

    def wait_loads(i):
        b, h = lax.div(i, heads), lax.rem(i, heads)
        settle(qg_buf.at[b, h], load_sem.at[0, b, h])
        settle(kv_buf.at[b, h], load_sem.at[1, b, h])

    def score_step(i, bufs):
        scores_buf, prob_grad_buf, peak_buf = bufs
        b, h = lax.div(i, heads), lax.rem(i, heads)
        keys = kv_buf[b, h, 0]
        values = kv_buf[b, h, 1]
        for n in range(blocks):
            span = pl.ds(n * query_block, query_block)
            scores = dot_nt(keys, qg_buf[b, h, 0, span, :])
            scores_buf[n] = scores
            peak_buf[n] = jnp.max(scores, axis=0, keepdims=True)
            prob_grad_buf[n] = dot_nt(values, qg_buf[b, h, 1, span, :])

    def grad_step(i, bufs):
        scores_buf, prob_grad_buf, peak_buf = bufs
        b, h = lax.div(i, heads), lax.rem(i, heads)
        key_grad = None
        for n in range(blocks):
            span = pl.ds(n * query_block, query_block)
            shifted = jnp.exp(scores_buf[n] - peak_buf[n])
            scale = 1.0 / jnp.sum(shifted, axis=0, keepdims=True)
            probs = shifted * scale
            probs_low = probs.astype(BF16)
            row_dot = jnp.sum(probs_low.astype(F32) * prob_grad_buf[n], axis=0, keepdims=True)
            score_low = (probs * (prob_grad_buf[n] - row_dot)).astype(BF16)
            value_term = dot_nn(probs_low, qg_buf[b, h, 1, span, :])
            key_term = dot_nn(score_low, qg_buf[b, h, 0, span, :])
            if key_grad is None:
                key_grad, value_grad = key_term, value_term
            else:
                key_grad, value_grad = key_grad + key_term, value_grad + value_term
        grads[:, pl.ds(pl.multiple_of(h * DK, DK), DK)] = key_grad.astype(BF16)
        grads[:, pl.ds(pl.multiple_of(inner + h * DK, DK), DK)] = value_grad.astype(BF16)

    even = (scores_even, prob_grad_even, peak_even)
    odd = (scores_odd, prob_grad_odd, peak_odd)

    def head_pair(i):
        wait_loads(i + 1)
        score_step(i + 1, odd)
        grad_step(i, even)
        following = jnp.minimum(i + 2, seqs * heads - 1)

        @pl.when(i + 2 < seqs * heads)
        def _():
            wait_loads(i + 2)

        score_step(following, even)
        grad_step(i + 1, odd)

    lower = z_me < chips // 2
    ahead = jnp.where(lower, chips - 1 - z_me, z_me)

    def order(j):
        rising = jnp.where(j < ahead, j, j - ahead)
        falling = chips - 1 - rising
        chip = jnp.where(lower == (j < ahead), falling, rising)
        return jnp.where(j == chips - 1, z_me, chip)

    def section_of(i):
        return lax.rem(s_me + i, sections)

    def piece(r):
        return pl.ds(r * piece_rows, piece_rows)

    def pair_copy(b, j):
        return pltpu.make_async_remote_copy(
            src_ref=part.at[b, j, CORES - 1 - c_me], dst_ref=pair_in.at[b, j],
            send_sem=pair_send, recv_sem=pair_recv.at[b, j],
            device_id={"tensor": partner}, device_id_type=MESH,
        )

    def section_copy(b, i, j, r):
        return pltpu.make_async_remote_copy(
            src_ref=part.at[b, j, c_me, section_of(i), piece(r)],
            dst_ref=section_in.at[b, i - 1, j, piece(r)],
            send_sem=section_send, recv_sem=section_recv.at[b, i - 1, j, r],
            device_id={"section": section_of(i)}, device_id_type=MESH,
        )

    def chain_copy(b, j, r):
        chip = order(j)
        right = chip > z_me
        target = jnp.where(right, z_me + 1, z_me - 1)
        slot = jnp.where(right | (chip != target), chip, chips)
        return pltpu.make_async_remote_copy(
            src_ref=line_out.at[b, j, piece(r)], dst_ref=line_in.at[b, slot, piece(r)],
            send_sem=line_send, recv_sem=line_recv.at[b, slot, r],
            device_id={"tensor": target * CORES + c_me}, device_id_type=MESH,
        )

    def chain_wait(b, slot, r):
        pltpu.make_async_remote_copy(
            src_ref=line_out.at[b, 0, piece(r)], dst_ref=line_in.at[b, slot, piece(r)],
            send_sem=line_send, recv_sem=line_recv.at[b, slot, r],
            device_id={"tensor": partner}, device_id_type=MESH,
        ).wait_recv()

    def stat_copies(src, dst, send, recv):
        return [
            pltpu.make_async_remote_copy(
                src_ref=src, dst_ref=dst.at[i - 1],
                send_sem=send, recv_sem=recv,
                device_id={"tensor": lax.rem(t_me + i, tensors)}, device_id_type=MESH,
            )
            for i in range(1, tensors)
        ]

    def square_copies():
        return stat_copies(square_out, square_in, square_send, square_recv)

    def cross_copies(b):
        return stat_copies(
            cross_out.at[b], cross_in.at[b], cross_send, cross_recv.at[b]
        )

    def lane_sums(x):
        total = dot_nt(jnp.ones((8, feats), F32), x, lax.Precision.HIGHEST)
        return total[0:1, :]

    def spread(row):
        return dot_tn(
            jnp.broadcast_to(row, (8, rows)), jnp.full((8, feats), 0.125, F32),
            lax.Precision.HIGHEST,
        )

    def loop(low, high, step):
        def run(i, carry):
            step(i)
            return carry

        lax.fori_loop(low, high, run, 0)

    def project(b, j):
        width = CORES * feats
        block = dot_nt(
            grads[...], w_buf[pl.ds(pl.multiple_of(order(j) * width, width), width), :]
        )
        for half in range(CORES):
            part[b, j, half] = block[:, half * feats : (half + 1) * feats].reshape(
                sections, rows, feats
            )
        pair_copy(b, j).start()

    def send_section(b, j):
        pair_copy(b, j).wait_recv()
        for i in range(1, sections):
            section = section_of(i)
            for r in range(pieces):
                part[b, j, c_me, section, piece(r)] += pair_in[b, j, section, piece(r)]
                section_copy(b, i, j, r).start()

    lead = 1 if chips > 1 else 0

    def project_all(b, between):
        def step(j):
            project(b, j)

            @pl.when(j == 1)
            def _():
                send_section(b, 0)

            @pl.when(j >= 3)
            def _():
                send_section(b, j - 2)

            between(j)

        loop(0, chips, step)

    def send_rest(b):
        loop(max(lead, chips - 2), chips, lambda j: send_section(b, j))

    def gather_piece(b, j, r):
        total = part[b, j, c_me, s_me, piece(r)] + pair_in[b, j, s_me, piece(r)]
        for i in range(1, sections):
            section_copy(b, i, j, r).wait_recv()
            total = total + section_in[b, i - 1, j, piece(r)]
        line_out[b, j, piece(r)] = total
        chip = order(j)
        behind = jnp.where(chip > z_me, z_me > 0, z_me < chips - 1)

        @pl.when((j < chips - 1) & behind)
        def _():
            chain_wait(b, chip, r)
            line_out[b, j, piece(r)] += line_in[b, chip, piece(r)]

        @pl.when(j < chips - 1)
        def _():
            chain_copy(b, j, r).start()

    def finish_sum(b):
        own = chips - 1
        for r in range(pieces):
            @pl.when(z_me > 0)
            def _():
                chain_wait(b, z_me, r)
                line_out[b, own, piece(r)] += line_in[b, z_me, piece(r)]

            @pl.when(z_me < chips - 1)
            def _():
                chain_wait(b, chips, r)
                line_out[b, own, piece(r)] += line_in[b, chips, piece(r)]

            out_ref[b, piece(r)] = gain[...] * line_out[b, own, piece(r)]
        cross_out[b] = lane_sums(out_ref[b] * hidden[b])
        for copy in cross_copies(b):
            copy.start()
        out_ref[b] = out_ref[b] * inverse_wide[b]

    def prepare_norm():
        settle(square_in, square_recv)
        for b in range(seqs):
            square = square_out[b]
            for i in range(tensors - 1):
                square = square + square_in[i, b]
            inverse = lax.rsqrt(square / model_width + EPSILON)
            inverse_wide[b] = spread(inverse)
            hidden_scaled[b] = hidden[b] * spread(inverse * inverse * inverse / model_width)

    def finish_norm(b):
        cross = cross_out[b]
        settle(cross_in.at[b], cross_recv.at[b])
        for i in range(tensors - 1):
            cross = cross + cross_in[b, i]
        out_ref[b] = out_ref[b] - hidden_scaled[b] * spread(cross)

    steps = heads // 2
    total_pieces = chips * pieces

    def gather_span(b, low, high):
        def step(n):
            gather_piece(b, lax.div(n, pieces), lax.rem(n, pieces))

        loop(jnp.minimum(low, total_pieces), jnp.minimum(high, total_pieces), step)

    delay = jnp.where(at_end, 0, 3)
    batch = max(pieces // 2, 1)

    def gather_until(b, point):
        low = jnp.maximum(point - delay, 0) * batch
        high = jnp.maximum(point + 1 - delay, 0) * batch
        gather_span(b, low, jnp.minimum(high, total_pieces - batch))

    points = steps + chips

    def sequence(b):
        def heads_step(j):
            head_pair(b * heads + 2 * j)

            @pl.when((b == 0) & (j == 0))
            def _():
                pl.semaphore_wait(barrier, tensors - 1 + sections - 1)

            @pl.when(b > 0)
            def _():
                @pl.when(j == 0)
                def _():
                    send_rest(b - 1)

                gather_until(b - 1, j)

        def between(j):
            @pl.when(b > 0)
            def _():
                gather_until(b - 1, steps + j)

        loop(0, steps, heads_step)

        @pl.when(b == 0)
        def _():
            for copy in small_copies:
                copy.wait()
            settle(w_buf, weight_sem)

        project_all(b, between)

        @pl.when(b == 0)
        def _():
            for i in range(seqs):
                square_out[i] = lane_sums(hidden[i] * hidden[i])
            for copy in square_copies():
                copy.start()

    wait_loads(0)
    score_step(0, even)
    loop(0, seqs, sequence)
    last = seqs - 1
    send_rest(last)
    if seqs > 1:
        done = jnp.minimum(jnp.maximum(points - delay, 0) * batch, total_pieces - batch)
        gather_span(last - 1, done, total_pieces)
    prepare_norm()
    gather_span(last, 0, total_pieces // 2)
    for b in range(seqs - 1):
        finish_sum(b)
    gather_span(last, total_pieces // 2, total_pieces)
    finish_sum(last)
    for b in range(seqs):
        finish_norm(b)

    settle(pair_in, pair_send)
    settle(section_in, section_send)
    settle(line_out.at[:, pl.ds(0, chips - 1)], line_send)
    settle(square_in, square_send)
    settle(cross_in, cross_send)


def per_device(
    sections, tensors,
    dec_queries, enc_keys, enc_values, out_grad, key_weight, value_weight, enc_hidden, enc_gain,
):
    _, seqs, dec_len, inner = dec_queries.shape
    enc_len = enc_keys.shape[2]
    heads = inner // DK
    model_width = key_weight.shape[1]
    chips = tensors // CORES
    feats = model_width // tensors
    rows = enc_len // sections
    dma = pltpu.SemaphoreType.DMA
    query_block = min(QUERY_BLOCK, dec_len)
    blocks = dec_len // query_block
    unit = [
        pltpu.VMEM((blocks, enc_len, query_block), F32),
        pltpu.VMEM((blocks, enc_len, query_block), F32),
        pltpu.VMEM((blocks, 1, query_block), F32),
    ]
    call = pl.pallas_call(
        functools.partial(body, sections, tensors, query_block),
        out_shape=jax.ShapeDtypeStruct((seqs, rows, feats), F32),
        in_specs=[pl.BlockSpec(memory_space=pl.ANY)] * 8,
        out_specs=pl.BlockSpec(memory_space=pltpu.VMEM),
        scratch_shapes=[
            pltpu.VMEM((seqs, heads, 2, dec_len, DK), BF16),
            pltpu.VMEM((seqs, heads, 2, enc_len, DK), BF16),
            pltpu.VMEM((model_width, 2 * inner), BF16),
            pltpu.VMEM((seqs, rows, feats), F32),
            pltpu.VMEM((1, feats), F32),
            pltpu.VMEM((enc_len, 2 * inner), BF16),
            *unit, *unit,
            pltpu.VMEM((seqs, chips, CORES, sections, rows, feats), F32),
            pltpu.VMEM((seqs, chips, sections, rows, feats), F32),
            pltpu.VMEM((seqs, sections - 1, chips, rows, feats), F32),
            pltpu.VMEM((seqs, chips, rows, feats), F32),
            pltpu.VMEM((seqs, chips + 1, rows, feats), F32),
            pltpu.VMEM((seqs, 1, rows), F32),
            pltpu.VMEM((tensors - 1, seqs, 1, rows), F32),
            pltpu.VMEM((seqs, 1, rows), F32),
            pltpu.VMEM((seqs, tensors - 1, 1, rows), F32),
            pltpu.VMEM((seqs, rows, feats), F32),
            pltpu.VMEM((seqs, rows, feats), F32),
            dma((2, seqs, heads)),
            dma(()),
            dma((2,)),
            dma(()),
            dma((seqs, chips)),
            dma(()),
            dma((seqs, sections - 1, chips, PIECES)),
            dma(()),
            dma((seqs, chips + 1, PIECES)),
            dma(()),
            dma(()),
            dma(()),
            dma((seqs,)),
        ],
        compiler_params=pltpu.CompilerParams(
            collective_id=0, has_side_effects=True, vmem_limit_bytes=60 * 1024 * 1024
        ),
    )
    return call(
        dec_queries, enc_keys, enc_values, out_grad, key_weight, value_weight,
        enc_hidden, enc_gain.reshape(1, feats),
    )


def solution(mesh):
    wide = P("section", "dp", None, "tensor")
    return jax.shard_map(
        functools.partial(per_device, mesh.shape["section"], mesh.shape["tensor"]),
        mesh=mesh,
        in_specs=(
            wide, wide, wide, wide,
            P("section", None, "tensor"),
            P("section", None, "tensor"),
            P("dp", "section", "tensor"),
            P("tensor"),
        ),
        out_specs=P("dp", "section", "tensor"),
        check_vma=False,
    )
```

time: 52.5 us -> 50.3 us (0.958)
  Pallas kernels: 50.7 us -> 48.5 us
    pallas_call x1, Pallas kernels: 50.7 us -> 48.5 us  [per_device(): call(dec_queries, enc_keys, enc_values, out_grad, key_weight, value_weigh...]
where the time goes in v2:
time: 50.3 us; the launch traced here: 50.2 us
  Pallas kernels  48.5 us (96%)
  local copies, waits for them, and re-layouts  1.67 us (3%)
    pallas_call x1, Pallas kernels, per_device(): call(dec_queries, enc_keys, enc_values, out_grad, key_weight, value_weigh...  48.5 us
    unnamed x1, local copies, waits for them, and re-layouts  1.67 us

profile of v2, /device:TPU:0, one launch (start us, length us, event | category | flops | bytes accessed | tf_op | source)
XLA Modules:
  0.0 50.2 jit_solution(7607045283011636532)
XLA Ops:
  0.0 48.5 %shard_map.82 = f32[2,256,128]{2,1,0:T(8,128)} custom-call(bf16[1,2,512,1024]{3,2,1,0:T(8,128)(2,1)} %q_hbm.1, bf16[1,2,512,1024]{3,2,1,0:T(8,128)(2,1)} %k_hbm.1, bf16[1,2,512,1024]{3,2,1,0:T(8,128)(2,1)} %v_hbm.1, bf16[1,2,512,1024]{3,2,1,0:T(8,128)(2,1)} %g_hbm.1, bf16[1,1024,1024]{2,1,0:T(8,128)(2,1)} %wk_hbm.1, bf16[1,1024,1024]{2,1,0:T(8,128)(2,1)} %wv_hbm.1, ...), custom_call_target="tpu_custom_call" | custom-call | tf_op jit(solution)/shard_map/pallas_call | solution.py:483
  48.5 1.7 %copy.10 = f32[2,256,128]{2,1,0:T(8,128)} copy(f32[2,256,128]{2,1,0:T(8,128)} %shard_map.82) | data formatting | bytes 524288

commit v3 on v2

--- a/solution.py
+++ b/solution.py
@@ -13,8 +13,8 @@
 MESH = pl.DeviceIdType.MESH
 F32 = jnp.float32
 BF16 = jnp.bfloat16
-QUERY_BLOCK = 256
-PIECES = 4
+QUERY_BLOCK = 128
+PIECES = 2
 
 
 def dot_nt(a, b, precision=None):
@@ -40,10 +40,11 @@
     qg_buf, kv_buf, w_buf, hidden, gain, grads,
     scores_even, prob_grad_even, peak_even, scores_odd, prob_grad_odd, peak_odd,
     part, pair_in, section_in, line_out, line_in,
-    square_out, square_in, cross_out, cross_in, inverse_wide, hidden_scaled,
+    square_out, square_in, cross_out, cross_in, inverse_gain, hidden_scaled, scaled_hidden, products,
     load_sem, weight_sem, small_sem,
     pair_send, pair_recv, section_send, section_recv, line_send, line_recv,
     square_send, square_recv, cross_send, cross_recv,
+    share_send, share_recv,
 ):
     seqs, heads, _, dec_len, _ = qg_buf.shape
     enc_len = kv_buf.shape[3]
@@ -161,6 +162,7 @@
         score_step(following, even)
         grad_step(i + 1, odd)
 
+    last = seqs - 1
     lower = z_me < chips // 2
     ahead = jnp.where(lower, chips - 1 - z_me, z_me)
 
@@ -209,6 +211,13 @@
             device_id={"tensor": partner}, device_id_type=MESH,
         ).wait_recv()
 
+    def share_copy(i):
+        return pltpu.make_async_remote_copy(
+            src_ref=scaled_hidden.at[z_me], dst_ref=scaled_hidden.at[z_me],
+            send_sem=share_send, recv_sem=share_recv,
+            device_id={"tensor": lax.rem(z_me + i, chips) * CORES + c_me}, device_id_type=MESH,
+        )
+
     def stat_copies(src, dst, send, recv):
         return [
             pltpu.make_async_remote_copy(
@@ -284,13 +293,15 @@
     def send_rest(b):
         loop(max(lead, chips - 2), chips, lambda j: send_section(b, j))
 
-    def gather_piece(b, j, r):
+    def gather_piece(b, j, r, tally=False):
         total = part[b, j, c_me, s_me, piece(r)] + pair_in[b, j, s_me, piece(r)]
         for i in range(1, sections):
             section_copy(b, i, j, r).wait_recv()
             total = total + section_in[b, i - 1, j, piece(r)]
         line_out[b, j, piece(r)] = total
         chip = order(j)
+        if tally:
+            products[piece(r)] += scaled_hidden[chip, piece(r)] * total
         behind = jnp.where(chip > z_me, z_me > 0, z_me < chips - 1)
 
         @pl.when((j < chips - 1) & behind)
@@ -315,20 +326,23 @@
                 chain_wait(b, chips, r)
                 line_out[b, own, piece(r)] += line_in[b, chips, piece(r)]
 
-            out_ref[b, piece(r)] = gain[...] * line_out[b, own, piece(r)]
-        cross_out[b] = lane_sums(out_ref[b] * hidden[b])
+            out_ref[b, piece(r)] = line_out[b, own, piece(r)] * inverse_gain[b, piece(r)]
+
+    def send_cross(b, terms):
+        cross_out[b] = lane_sums(terms)
         for copy in cross_copies(b):
             copy.start()
-        out_ref[b] = out_ref[b] * inverse_wide[b]
 
     def prepare_norm():
         settle(square_in, square_recv)
+        settle(scaled_hidden.at[pl.ds(0, chips - 1)], share_recv)
+        products[...] = jnp.zeros_like(products)
         for b in range(seqs):
             square = square_out[b]
             for i in range(tensors - 1):
                 square = square + square_in[i, b]
             inverse = lax.rsqrt(square / model_width + EPSILON)
-            inverse_wide[b] = spread(inverse)
+            inverse_gain[b] = gain[...] * spread(inverse)
             hidden_scaled[b] = hidden[b] * spread(inverse * inverse * inverse / model_width)
 
     def finish_norm(b):
@@ -341,9 +355,9 @@
     steps = heads // 2
     total_pieces = chips * pieces
 
-    def gather_span(b, low, high):
+    def gather_span(b, low, high, tally=False):
         def step(n):
-            gather_piece(b, lax.div(n, pieces), lax.rem(n, pieces))
+            gather_piece(b, lax.div(n, pieces), lax.rem(n, pieces), tally)
 
         loop(jnp.minimum(low, total_pieces), jnp.minimum(high, total_pieces), step)
 
@@ -363,7 +377,12 @@
 
             @pl.when((b == 0) & (j == 0))
             def _():
+                for copy in small_copies:
+                    copy.wait()
+                scaled_hidden[z_me] = gain[...] * hidden[last]
                 pl.semaphore_wait(barrier, tensors - 1 + sections - 1)
+                for i in range(1, chips):
+                    share_copy(i).start()
 
             @pl.when(b > 0)
             def _():
@@ -382,8 +401,6 @@
 
         @pl.when(b == 0)
         def _():
-            for copy in small_copies:
-                copy.wait()
             settle(w_buf, weight_sem)
 
         project_all(b, between)
@@ -398,16 +415,17 @@
     wait_loads(0)
     score_step(0, even)
     loop(0, seqs, sequence)
-    last = seqs - 1
     send_rest(last)
     if seqs > 1:
         done = jnp.minimum(jnp.maximum(points - delay, 0) * batch, total_pieces - batch)
         gather_span(last - 1, done, total_pieces)
     prepare_norm()
-    gather_span(last, 0, total_pieces // 2)
-    for b in range(seqs - 1):
+    gather_span(last, 0, total_pieces // 2, True)
+    for b in range(last):
         finish_sum(b)
-    gather_span(last, total_pieces // 2, total_pieces)
+        send_cross(b, line_out[b, chips - 1] * (gain[...] * hidden[b]))
+    gather_span(last, total_pieces // 2, total_pieces, True)
+    send_cross(last, products[...])
     finish_sum(last)
     for b in range(seqs):
         finish_norm(b)
@@ -417,6 +435,7 @@
     settle(line_out.at[:, pl.ds(0, chips - 1)], line_send)
     settle(square_in, square_send)
     settle(cross_in, cross_send)
+    settle(scaled_hidden.at[pl.ds(0, chips - 1)], share_send)
 
 
 def per_device(
@@ -462,6 +481,8 @@
             pltpu.VMEM((seqs, tensors - 1, 1, rows), F32),
             pltpu.VMEM((seqs, rows, feats), F32),
             pltpu.VMEM((seqs, rows, feats), F32),
+            pltpu.VMEM((chips, rows, feats), F32),
+            pltpu.VMEM((rows, feats), F32),
             dma((2, seqs, heads)),
             dma(()),
             dma((2,)),
@@ -475,6 +496,8 @@
             dma(()),
             dma(()),
             dma((seqs,)),
+            dma(()),
+            dma(()),
         ],
         compiler_params=pltpu.CompilerParams(
             collective_id=0, has_side_effects=True, vmem_limit_bytes=60 * 1024 * 1024

time: 50.3 us -> 46.7 us (0.928)
  Pallas kernels: 48.5 us -> 44.9 us
    pallas_call x1, Pallas kernels: 48.5 us -> 44.9 us  [per_device(): call(dec_queries, enc_keys, enc_values, out_grad, key_weight, value_weigh...]
where the time goes in v3:
time: 46.7 us; the launch traced here: 46.6 us
  Pallas kernels  44.9 us (96%)
  local copies, waits for them, and re-layouts  1.67 us (4%)
    pallas_call x1, Pallas kernels, per_device(): call(dec_queries, enc_keys, enc_values, out_grad, key_weight, value_weigh...  44.9 us
    unnamed x1, local copies, waits for them, and re-layouts  1.67 us

profile of v3, /device:TPU:0, one launch (start us, length us, event | category | flops | bytes accessed | tf_op | source)
XLA Modules:
  0.0 46.6 jit_solution(17162931788528803772)
XLA Ops:
  0.0 44.9 %shard_map.82 = f32[2,256,128]{2,1,0:T(8,128)} custom-call(bf16[1,2,512,1024]{3,2,1,0:T(8,128)(2,1)} %q_hbm.1, bf16[1,2,512,1024]{3,2,1,0:T(8,128)(2,1)} %k_hbm.1, bf16[1,2,512,1024]{3,2,1,0:T(8,128)(2,1)} %v_hbm.1, bf16[1,2,512,1024]{3,2,1,0:T(8,128)(2,1)} %g_hbm.1, bf16[1,1024,1024]{2,1,0:T(8,128)(2,1)} %wk_hbm.1, bf16[1,1024,1024]{2,1,0:T(8,128)(2,1)} %wv_hbm.1, ...), custom_call_target="tpu_custom_call" | custom-call | tf_op jit(solution)/shard_map/pallas_call | solution.py:506
  44.9 1.7 %copy.10 = f32[2,256,128]{2,1,0:T(8,128)} copy(f32[2,256,128]{2,1,0:T(8,128)} %shard_map.82) | data formatting | bytes 524288

commit v4 on v3

--- a/solution.py
+++ b/solution.py
@@ -500,13 +500,14 @@
             dma(()),
         ],
         compiler_params=pltpu.CompilerParams(
-            collective_id=0, has_side_effects=True, vmem_limit_bytes=60 * 1024 * 1024
+            collective_id=0, has_side_effects=True, vmem_limit_bytes=48 * 1024 * 1024
         ),
     )
-    return call(
+    operands = (
         dec_queries, enc_keys, enc_values, out_grad, key_weight, value_weight,
         enc_hidden, enc_gain.reshape(1, feats),
     )
+    return call(*(pltpu.with_memory_space_constraint(x, pltpu.HBM) for x in operands))
 
 
 def solution(mesh):

time: 46.7 us -> 45.1 us (0.966)
  local copies, waits for them, and re-layouts: 1.67 us -> 0.71 us
  Pallas kernels: 44.9 us -> 44.2 us
    unnamed x1, local copies, waits for them, and re-layouts: 1.67 us -> 0.71 us
    pallas_call x1, Pallas kernels: 44.9 us -> 44.2 us  [per_device(): call(*(pltpu.with_memory_space_constraint(x, pltpu.HBM) for x in operands))]
where the time goes in v4:
time: 45.1 us; the launch traced here: 44.9 us
  Pallas kernels  44.2 us (98%)
  local copies, waits for them, and re-layouts  0.71 us (2%)
    pallas_call x1, Pallas kernels, per_device(): call(*(pltpu.with_memory_space_constraint(x, pltpu.HBM) for x in operands))  44.2 us

profile of v4, /device:TPU:0, one launch (start us, length us, event | category | flops | bytes accessed | tf_op | source)
XLA Modules:
  0.0 44.9 jit_solution(8641160528053814158)
XLA Ops:
  0.0 44.2 %shard_map.82 = f32[2,256,128]{2,1,0:T(8,128)S(1)} custom-call(bf16[1,2,512,1024]{3,2,1,0:T(8,128)(2,1)} %q_hbm.1, bf16[1,2,512,1024]{3,2,1,0:T(8,128)(2,1)} %k_hbm.1, bf16[1,2,512,1024]{3,2,1,0:T(8,128)(2,1)} %v_hbm.1, bf16[1,2,512,1024]{3,2,1,0:T(8,128)(2,1)} %g_hbm.1, bf16[1,1024,1024]{2,1,0:T(8,128)(2,1)} %wk_hbm.1, bf16[1,1024,1024]{2,1,0:T(8,128)(2,1)} %wv_hbm.1, ...), custom_call_target="tpu_custom_call" | custom-call | tf_op jit(solution)/shard_map/pallas_call | solution.py:510
  44.2 0.7 %copy.10 = f32[2,256,128]{2,1,0:T(8,128)} copy(f32[2,256,128]{2,1,0:T(8,128)S(1)} %shard_map.82) | data formatting | bytes 524288

commit v5 on v4

--- a/solution.py
+++ b/solution.py
@@ -313,7 +313,7 @@
         def _():
             chain_copy(b, j, r).start()
 
-    def finish_sum(b):
+    def finish_sum(b, finish):
         own = chips - 1
         for r in range(pieces):
             @pl.when(z_me > 0)
@@ -326,7 +326,7 @@
                 chain_wait(b, chips, r)
                 line_out[b, own, piece(r)] += line_in[b, chips, piece(r)]
 
-            out_ref[b, piece(r)] = line_out[b, own, piece(r)] * inverse_gain[b, piece(r)]
+            finish(r)
 
     def send_cross(b, terms):
         cross_out[b] = lane_sums(terms)
@@ -335,8 +335,6 @@
 
     def prepare_norm():
         settle(square_in, square_recv)
-        settle(scaled_hidden.at[pl.ds(0, chips - 1)], share_recv)
-        products[...] = jnp.zeros_like(products)
         for b in range(seqs):
             square = square_out[b]
             for i in range(tensors - 1):
@@ -345,12 +343,16 @@
             inverse_gain[b] = gain[...] * spread(inverse)
             hidden_scaled[b] = hidden[b] * spread(inverse * inverse * inverse / model_width)
 
-    def finish_norm(b):
+    def correction(b):
         cross = cross_out[b]
         settle(cross_in.at[b], cross_recv.at[b])
         for i in range(tensors - 1):
             cross = cross + cross_in[b, i]
-        out_ref[b] = out_ref[b] - hidden_scaled[b] * spread(cross)
+        hidden_scaled[b] = hidden_scaled[b] * spread(cross)
+
+    def write(b, r):
+        total = line_out[b, chips - 1, piece(r)]
+        out_ref[b, piece(r)] = total * inverse_gain[b, piece(r)] - hidden_scaled[b, piece(r)]
 
     steps = heads // 2
     total_pieces = chips * pieces
@@ -361,13 +363,17 @@
 
         loop(jnp.minimum(low, total_pieces), jnp.minimum(high, total_pieces), step)
 
-    delay = jnp.where(at_end, 0, 3)
-    batch = max(pieces // 2, 1)
+    end_points = (0, 1, 2, 2, 3, 4, 6)
+    mid_points = (2, 3, 5, 6, 6, 7)
+
+    def reached(point):
+        def count(starts):
+            return sum(jnp.where(point >= start, 1, 0) for start in starts)
+
+        return jnp.where(at_end, count(end_points), count(mid_points))
 
     def gather_until(b, point):
-        low = jnp.maximum(point - delay, 0) * batch
-        high = jnp.maximum(point + 1 - delay, 0) * batch
-        gather_span(b, low, jnp.minimum(high, total_pieces - batch))
+        gather_span(b, reached(point - 1), reached(point))
 
     points = steps + chips
 
@@ -405,30 +411,32 @@
 
         project_all(b, between)
 
-        @pl.when(b == 0)
-        def _():
-            for i in range(seqs):
-                square_out[i] = lane_sums(hidden[i] * hidden[i])
-            for copy in square_copies():
-                copy.start()
-
     wait_loads(0)
     score_step(0, even)
     loop(0, seqs, sequence)
     send_rest(last)
     if seqs > 1:
-        done = jnp.minimum(jnp.maximum(points - delay, 0) * batch, total_pieces - batch)
+        done = jnp.minimum(reached(points - 1), total_pieces)
         gather_span(last - 1, done, total_pieces)
-    prepare_norm()
+    for b in range(seqs):
+        square_out[b] = lane_sums(hidden[b] * hidden[b])
+    for copy in square_copies():
+        copy.start()
+    products[...] = jnp.zeros_like(products)
+    settle(scaled_hidden.at[pl.ds(0, chips - 1)], share_recv)
     gather_span(last, 0, total_pieces // 2, True)
     for b in range(last):
-        finish_sum(b)
+        finish_sum(b, lambda r: None)
         send_cross(b, line_out[b, chips - 1] * (gain[...] * hidden[b]))
     gather_span(last, total_pieces // 2, total_pieces, True)
     send_cross(last, products[...])
-    finish_sum(last)
-    for b in range(seqs):
-        finish_norm(b)
+    prepare_norm()
+    for b in range(last):
+        correction(b)
+        for r in range(pieces):
+            write(b, r)
+    correction(last)
+    finish_sum(last, lambda r: write(last, r))
 
     settle(pair_in, pair_send)
     settle(section_in, section_send)

time: 45.1 us -> 45.1 us (level)
  no operation moved by 1% of the time
where the time goes in v5:
time: 45.1 us; the launch traced here: 44.9 us
  Pallas kernels  44.2 us (98%)
  local copies, waits for them, and re-layouts  0.71 us (2%)
    pallas_call x1, Pallas kernels, per_device(): call(*(pltpu.with_memory_space_constraint(x, pltpu.HBM) for x in operands))  44.2 us

profile of v5, /device:TPU:0, one launch (start us, length us, event | category | flops | bytes accessed | tf_op | source)
XLA Modules:
  0.0 44.9 jit_solution(13393362412852169666)
XLA Ops:
  0.0 44.2 %shard_map.82 = f32[2,256,128]{2,1,0:T(8,128)S(1)} custom-call(bf16[1,2,512,1024]{3,2,1,0:T(8,128)(2,1)} %q_hbm.1, bf16[1,2,512,1024]{3,2,1,0:T(8,128)(2,1)} %k_hbm.1, bf16[1,2,512,1024]{3,2,1,0:T(8,128)(2,1)} %v_hbm.1, bf16[1,2,512,1024]{3,2,1,0:T(8,128)(2,1)} %g_hbm.1, bf16[1,1024,1024]{2,1,0:T(8,128)(2,1)} %wk_hbm.1, bf16[1,1024,1024]{2,1,0:T(8,128)(2,1)} %wv_hbm.1, ...), custom_call_target="tpu_custom_call" | custom-call | tf_op jit(solution)/shard_map/pallas_call | solution.py:518
  44.2 0.7 %copy.10 = f32[2,256,128]{2,1,0:T(8,128)} copy(f32[2,256,128]{2,1,0:T(8,128)S(1)} %shard_map.82) | data formatting | bytes 524288
